TPU v7x, 32 devices: a whole 2x2x4 slice. The times are simulated.
32 devices in a mesh: groups: 1, tok: 32 (over z, y, x, core).
Axes of the slice: x: 2, y: 2, z: 4, core: 2. Of those that a mesh axis runs over, the one named last changes fastest.
Arguments:
- queries: bfloat16 [4096, 2560], P(('groups', 'tok')), may hold values from -5 to 5
- key_rows: bfloat16 [4096, 2560], P(('groups', 'tok')), may hold values from -5 to 5
- value_rows: bfloat16 [4096, 2560], P(('groups', 'tok')), may hold values from -6 to 6
- learn_rates: float32 [4096, 8], P(('groups', 'tok')), may hold values from 0.0002 to 0.002
- frame_order: int32 [4096], P('groups'), may hold values from 0 to 4095, as said below
- window_ids: int32 [4096], P('groups'), may hold values from 0 to 7, never falling along the last dimension, each value on 1 to 2048 neighbouring positions
- fast_init: bfloat16 [640, 3, 2560], replicated, may hold values from -0.3125 to 0.3125
- norm_gain: float32 [2560], replicated, may hold values from 0.5 to 1.5
Outputs:
- layer_out: bfloat16 [4096, 2560], P(('groups', 'tok'))
Inputs may be any that keep to these rules, and one draw needn't show every extreme that they name: frame_order[i] is the sequence position of the token stored at row i; every position appears once, and every aligned block of 128 stored rows holds exactly 4 positions of every aligned block of 128 positions.
All inputs are finite; a program needn't handle non-finite values.
Results may differ from a plain program's by a relative error of at most 0.025.
Values may be sent and summed in bfloat16 or wider, within the bound.
A program may use at most 192 MiB of HBM per device.

v0:
```python
import jax
import jax.numpy as jnp
from jax import lax
from jax.sharding import PartitionSpec as P

HEADS = 8
HEAD_DIM = 320
ATT_DIM = 128
WINDOW = 1024
WIDTH = 2560
ATT_HEADS = 20


epsilon = 1e-06


def shifted(block, axis, distance):
    devices = range(lax.axis_size(axis))
    route = [(i - distance, i) for i in devices if i - distance in devices]
    return lax.ppermute(block, axis, route)


def head_view(rows):
    return rows.reshape(rows.shape[0], HEADS, HEAD_DIM)


def matrix_view(weight_rows, which):
    return weight_rows[:, which].reshape(weight_rows.shape[0], HEADS, HEAD_DIM)


def fast_grads(key_block, value_block, rate_block, weight_rows):
    row_count = weight_rows.shape[0]
    key_heads = head_view(key_block)
    target = (head_view(value_block).astype(jnp.float32) * rate_block[:, :, None]).astype(
        jnp.bfloat16
    )
    gate = jnp.einsum(
        "thd,jhd->thj", key_heads, matrix_view(weight_rows, 0), preferred_element_type=jnp.float32
    )
    upward = jnp.einsum(
        "thd,jhd->thj", key_heads, matrix_view(weight_rows, 1), preferred_element_type=jnp.float32
    )
    backward = jnp.einsum(
        "thd,jhd->thj", target, matrix_view(weight_rows, 2), preferred_element_type=jnp.float32
    )
    sigmoid = jax.nn.sigmoid(gate)
    active = gate * sigmoid
    product = (active * upward).astype(jnp.bfloat16)
    delta_gate = (backward * upward * sigmoid * (1.0 + gate * (1.0 - sigmoid))).astype(jnp.bfloat16)
    delta_upper = (backward * active).astype(jnp.bfloat16)
    grad_gate = jnp.einsum(
        "thj,thd->jhd", delta_gate, key_heads, preferred_element_type=jnp.float32
    )
    grad_upper = jnp.einsum(
        "thj,thd->jhd", delta_upper, key_heads, preferred_element_type=jnp.float32
    )
    grad_down = jnp.einsum("thj,thd->jhd", product, target, preferred_element_type=jnp.float32)
    return jnp.stack(
        [
            grad_gate.reshape(row_count, WIDTH),
            grad_upper.reshape(row_count, WIDTH),
            grad_down.reshape(row_count, WIDTH),
        ],
        axis=1,
    )


def renormed(base_rows, grads):
    start_rows = base_rows.astype(jnp.float32)
    update = start_rows + grads
    shaped = update.reshape(update.shape[0], 3, HEADS, HEAD_DIM)
    anchor = start_rows.reshape(update.shape[0], 3, HEADS, HEAD_DIM)
    scaling = jnp.sqrt(jnp.sum(anchor * anchor, axis=-1, keepdims=True) + epsilon) / jnp.sqrt(
        jnp.sum(shaped * shaped, axis=-1, keepdims=True) + epsilon
    )
    return (shaped * scaling).reshape(update.shape).astype(jnp.bfloat16)


def fast_apply(query_block, weight_rows):
    query_heads = head_view(query_block)
    gate = jnp.einsum(
        "thd,jhd->thj", query_heads, matrix_view(weight_rows, 0), preferred_element_type=jnp.float32
    )
    upward = jnp.einsum(
        "thd,jhd->thj", query_heads, matrix_view(weight_rows, 1), preferred_element_type=jnp.float32
    )
    product = (jax.nn.silu(gate) * upward).astype(jnp.bfloat16)
    result = jnp.einsum(
        "thj,jhd->thd", product, matrix_view(weight_rows, 2), preferred_element_type=jnp.float32
    )
    return result.reshape(query_block.shape[0], WIDTH)


def window_attention(query_seq, key_ext, value_ext, allowed):

    def one_head(head, output):
        offset = head * ATT_DIM
        query_part = lax.dynamic_slice_in_dim(query_seq, offset, ATT_DIM, 1)
        key_part = lax.dynamic_slice_in_dim(key_ext, offset, ATT_DIM, 1)
        value_part = lax.dynamic_slice_in_dim(value_ext, offset, ATT_DIM, 1)
        scores = jnp.einsum(
            "td,sd->ts", query_part, key_part, preferred_element_type=jnp.float32
        ) * ATT_DIM ** (-0.5)
        scores = jnp.where(allowed, scores, -1e30)
        peak = jnp.max(scores, axis=1, keepdims=True)
        weights = jnp.exp(scores - peak)
        total = jnp.sum(weights, axis=1, keepdims=True)
        mixed = (
            jnp.dot(weights.astype(jnp.bfloat16), value_part, preferred_element_type=jnp.float32)
            / total
        )
        return lax.dynamic_update_slice_in_dim(output, mixed, offset, 1)

    return lax.fori_loop(0, ATT_HEADS, one_head, jnp.zeros(query_seq.shape, jnp.float32))


def shards(
    queries, key_rows, value_rows, learn_rates, frame_order, window_ids, fast_init, norm_gain
):
    tok_dev = queries.shape[0]
    token_total = window_ids.shape[0]
    sections = lax.axis_size("tok")
    device_rank = lax.axis_index("tok")
    slot_count = tok_dev // sections
    counter = jnp.arange(tok_dev, dtype=jnp.int32)
    local_order = lax.dynamic_slice_in_dim(frame_order, device_rank * tok_dev, tok_dev, 0)
    send_rank = jnp.argsort(local_order // tok_dev * tok_dev + counter)
    send_query = queries[send_rank].reshape(sections, slot_count, WIDTH)
    send_key = key_rows[send_rank].reshape(sections, slot_count, WIDTH)
    send_value = value_rows[send_rank].reshape(sections, slot_count, WIDTH)
    arrived = (
        lax.all_to_all(send_query, "tok", split_axis=0, concat_axis=0, tiled=True),
        lax.all_to_all(send_key, "tok", split_axis=0, concat_axis=0, tiled=True),
        lax.all_to_all(send_value, "tok", split_axis=0, concat_axis=0, tiled=True),
    )
    all_order = frame_order.reshape(sections, tok_dev)
    ranked = jnp.argsort(all_order // tok_dev * tok_dev + counter[None, :], axis=1)
    arranged = jnp.take_along_axis(all_order, ranked, axis=1)
    landing = lax.dynamic_slice_in_dim(arranged, device_rank * slot_count, slot_count, 1).reshape(
        -1
    )
    placing = jnp.argsort(landing - device_rank * tok_dev)
    query_seq = arrived[0].reshape(tok_dev, WIDTH)[placing]
    key_seq = arrived[1].reshape(tok_dev, WIDTH)[placing]
    value_seq = arrived[2].reshape(tok_dev, WIDTH)[placing]
    local_grads = fast_grads(key_rows, value_rows, learn_rates, fast_init)
    grads = lax.psum(local_grads.astype(jnp.bfloat16), "tok").astype(jnp.float32)
    fresh = renormed(fast_init, grads)
    fast_out = fast_apply(query_seq, fresh)
    half_span = WINDOW // 2
    edge_rows = min(half_span, tok_dev)
    hop_count = half_span // edge_rows
    low_edge = jnp.stack([key_seq, value_seq])
    high_edge = jnp.stack([key_seq, value_seq])
    before_parts = []
    after_parts = []
    for distance in range(1, hop_count + 1):
        before_parts.insert(0, shifted(low_edge, "tok", distance))
        after_parts.append(shifted(high_edge, "tok", -distance))
    key_ext = jnp.concatenate(
        [part_rows[0] for part_rows in before_parts]
        + [key_seq]
        + [part_rows[0] for part_rows in after_parts],
        axis=0,
    )
    value_ext = jnp.concatenate(
        [part_rows[1] for part_rows in before_parts]
        + [value_seq]
        + [part_rows[1] for part_rows in after_parts],
        axis=0,
    )
    span = tok_dev + 2 * half_span
    begin = device_rank * tok_dev
    ids_pad = jnp.pad(window_ids, (half_span, half_span), constant_values=-1)
    key_ids = lax.dynamic_slice_in_dim(ids_pad, begin, span, 0)
    query_ids = lax.dynamic_slice_in_dim(window_ids, begin, tok_dev, 0)
    query_pos = begin + counter
    key_pos = begin - half_span + jnp.arange(span, dtype=jnp.int32)
    allowed = (
        (key_pos[None, :] >= 0)
        & (key_pos[None, :] < token_total)
        & (jnp.abs(query_pos[:, None] - key_pos[None, :]) < half_span)
        & (query_ids[:, None] == key_ids[None, :])
    )
    attended = window_attention(query_seq, key_ext, value_ext, allowed)
    combined = fast_out + attended
    mean_square = jnp.mean(combined * combined, axis=1, keepdims=True)
    return (combined * lax.rsqrt(mean_square + epsilon) * norm_gain).astype(jnp.bfloat16)


def solution(mesh):
    return jax.shard_map(
        shards,
        mesh=mesh,
        in_specs=(
            P(("groups", "tok"), None),
            P(("groups", "tok"), None),
            P(("groups", "tok"), None),
            P(("groups", "tok"), None),
            P("groups"),
            P("groups"),
            P(),
            P(),
        ),
        out_specs=P(("groups", "tok"), None),
        check_vma=False,
    )
```

profile of v0, /device:TPU:0, one launch (start us, length us, event | category | flops | bytes accessed | tf_op | source)
XLA Modules:
  0.0 521.4 jit_solution(8994565235633225250)
XLA Ops:
  14.6 7.3 %all-to-all-start.2 = ((bf16[32,4,2560]{2,1,0:T(4,128)(2,1)}), bf16[32,4,2560]{2,1,0:T(4,128)(2,1)S(1)}, u32[]{:S(2)}, u32[]{:S(2)}) async-start(bf16[32,4,2560]{2,1,0:T(4,128)(2,1)} %reshape.104), calls=%async_computation.2 | async-start | bytes 1310720 | tf_op jit(solution)/shard_map/all_to_all | solution.py:134
  23.2 7.1 %fusion.67 = (bf16[640,1,2560]{2,0,1:T(8,128)(2,1)}, bf16[640,1,2560]{2,0,1:T(8,128)(2,1)}, bf16[640,1,2560]{2,0,1:T(8,128)(2,1)}) fusion(bf16[640,3,2560]{2,0,1:T(8,128)(2,1)} %param.16), kind=kLoop, calls=%fused_computation.132 | loop fusion | bytes 19660800 | tf_op jit(solution)/shard_map/slice | solution.py:28
  30.3 5.7 %copy.30 = bf16[640,1,2560]{0,2,1:T(8,128)(2,1)} copy(bf16[640,1,2560]{2,0,1:T(8,128)(2,1)} %get-tuple-element.179) | data formatting | bytes 6553600 | tf_op jit(solution)/shard_map/slice | solution.py:28
  36.3 5.6 %copy.33 = bf16[640,1,2560]{0,2,1:T(8,128)(2,1)} copy(bf16[640,1,2560]{2,0,1:T(8,128)(2,1)} %get-tuple-element.178) | data formatting | bytes 6553600 | tf_op jit(solution)/shard_map/slice | solution.py:28
  42.0 4.6 fusion.68
  51.2 5.7 %copy.29 = bf16[640,1,2560]{0,2,1:T(8,128)(2,1)} copy(bf16[640,1,2560]{2,0,1:T(8,128)(2,1)} %get-tuple-element.177) | data formatting | bytes 6553600 | tf_op jit(solution)/shard_map/slice | solution.py:28
  65.5 5.8 %all-to-all-start.1 = ((bf16[32,4,2560]{2,1,0:T(4,128)(2,1)}), bf16[32,4,2560]{2,1,0:T(4,128)(2,1)S(1)}, u32[]{:S(2)}, u32[]{:S(2)}) async-start(bf16[32,4,2560]{2,1,0:T(4,128)(2,1)} %reshape.102), calls=%async_computation.1 | async-start | bytes 1310720 | tf_op jit(solution)/shard_map/all_to_all | solution.py:133
  71.4 5.3 %convolution_convert_fusion.2 = bf16[8,320,640]{2,1,0:T(8,128)(2,1)} fusion(f32[8,640,128]{1,2,0:T(8,128)} %fusion.68, bf16[128,8,320]{0,2,1:T(8,128)(2,1)S(1)} %bitcast.202, f32[128,8]{0,1:T(8,128)S(1)} %copy-done.17, f32[8,640,128]{1,2,0:T(8,128)} %fusion.69), kind=kOutput, calls=%fused_computation.54 | convolution fusion | flops 425984000 | bytes 9179136 | tf_op jit(solution)/shard_map/thj,thd->jhd/dot_general | solution.py:57
  79.4 25.6 %gather_fusion.6 = s32[4096]{0:T(1024)S(1)} fusion(s32[32,128]{1,0:T(8,128)S(1)} %bitcast.181, s32[4096]{0:T(1024)S(1)} %fusion.59), kind=kCustom, calls=%fused_computation.6 | custom fusion | bytes 65536 | tf_op jit(solution)/shard_map/jit(take_along_axis)/gather | solution.py:138
  109.0 5.8 %all-to-all-start = ((bf16[32,4,2560]{2,1,0:T(4,128)(2,1)}), bf16[32,4,2560]{2,1,0:T(4,128)(2,1)S(1)}, u32[]{:S(2)}, u32[]{:S(2)}) async-start(bf16[32,4,2560]{2,1,0:T(4,128)(2,1)} %reshape.96), calls=%async_computation | async-start | bytes 1310720 | tf_op jit(solution)/shard_map/all_to_all | solution.py:132
  117.2 5.0 collective-permute-start
  129.7 4.7 pad_maximum_fusion
  134.5 14.0 %copy.27 = bf16[640,3,2560]{0,2,1:T(8,128)(2,1)} copy(bf16[640,3,2560]{2,0,1:T(8,128)(2,1)} %param.16) | data formatting | bytes 19660800 | tf_op args[6]
  157.1 71.9 %collective-permute-done = bf16[2,128,2560]{2,1,0:T(8,128)(2,1)} collective-permute-done((bf16[2,128,2560]{2,1,0:T(8,128)(2,1)}, bf16[2,128,2560]{2,1,0:T(8,128)(2,1)}, u32[]{:S(2)}, u32[]{:S(2)}) %collective-permute-start) | collective-permute-done | bytes 1310752 | tf_op jit(solution)/shard_map/ppermute | solution.py:20
  239.9 29.5 %collective-permute-done.5 = bf16[2,128,2560]{2,1,0:T(8,128)(2,1)S(1)} collective-permute-done((bf16[2,128,2560]{2,1,0:T(8,128)(2,1)}, bf16[2,128,2560]{2,1,0:T(8,128)(2,1)S(1)}, u32[]{:S(2)}, u32[]{:S(2)}) %collective-permute-start.5) | collective-permute-done | bytes 1310752 | tf_op jit(solution)/shard_map/ppermute | solution.py:20
  269.4 12.4 %collective-permute-done.6 = bf16[2,128,2560]{2,1,0:T(8,128)(2,1)S(1)} collective-permute-done((bf16[2,128,2560]{2,1,0:T(8,128)(2,1)}, bf16[2,128,2560]{2,1,0:T(8,128)(2,1)S(1)}, u32[]{:S(2)}, u32[]{:S(2)}) %collective-permute-start.6) | collective-permute-done | bytes 1310752 | tf_op jit(solution)/shard_map/ppermute | solution.py:20
  281.9 15.0 %collective-permute-done.7 = bf16[2,128,2560]{2,1,0:T(8,128)(2,1)S(1)} collective-permute-done((bf16[2,128,2560]{2,1,0:T(8,128)(2,1)}, bf16[2,128,2560]{2,1,0:T(8,128)(2,1)S(1)}, u32[]{:S(2)}, u32[]{:S(2)}) %collective-permute-start.7) | collective-permute-done | bytes 1310752 | tf_op jit(solution)/shard_map/ppermute | solution.py:20
  301.4 59.8 %while.14 = (s32[]{:T(128)}, f32[128,2560]{1,0:T(8,128)S(1)}, bf16[128,2560]{1,0:T(8,128)(2,1)S(1)}, bf16[1152,2560]{1,0:T(8,128)(2,1)}, bf16[1152,2560]{1,0:T(8...) while((s32[]{:T(128)}, f32[128,2560]{1,0:T(8,128)S(1)}, ...), condition=%wide.region_9.10_spmd.clone, body=%wide.region_6.9_spmd.clone.sunk | while | flops 77430528 | bytes 2481851 | solution.py:114
  361.2 93.6 %all-reduce.3.cloned.1.call-done = bf16[640,3,2560]{0,2,1:T(8,128)(2,1)} async-done(((bf16[640,3,2560]{0,2,1:T(8,128)(2,1)}), bf16[640,3,2560]{0,2,1:T(8,128)(2,1)}) %all-reduce.3.cloned.1.call-update) | async-done | bytes 9830416 | tf_op jit(solution)/shard_map/psum | solution.py:147
  454.8 19.8 %convert_multiply_fusion = (f32[640,3,2560]{0,2,1:T(8,128)}, f32[640,3,2560]{0,2,1:T(8,128)}) fusion(bf16[640,3,2560]{0,2,1:T(8,128)(2,1)} %copy.27, bf16[640,3,2560]{0,2,1:T(8,128)(2,1)} %all-reduce.3.cloned.1.call-done), kind=kLoop, calls=%fused_computation.24 | loop fusion | flops 24576000 | bytes 58982400 | tf_op jit(solution)/shard_map/mul | solution.py:73
  474.6 7.6 %reduce_sum.41 = f32[640,3,8]{0,2,1:T(8,128)S(1)} reduce(f32[640,3,8,320]{0,3,2,1:T(8,128)} %bitcast.183, f32[]{:T(128)} %constant.110.clone.1), dimensions={3}, to_apply=%region_2.3 | reduce | flops 4899840 | bytes 19722244 | tf_op jit(solution)/shard_map/reduce_sum | solution.py:74
  482.2 7.6 %reduce_sum.40 = f32[640,3,8]{0,2,1:T(8,128)S(1)} reduce(f32[640,3,8,320]{0,3,2,1:T(8,128)} %bitcast.182, f32[]{:T(128)} %constant.110.clone.1), dimensions={3}, to_apply=%region_1.2 | reduce | flops 4899840 | bytes 19722244 | tf_op jit(solution)/shard_map/reduce_sum | solution.py:73
  489.8 8.7 %fusion.15 = bf16[640,3,2560]{0,2,1:T(8,128)(2,1)S(1)} fusion(bf16[640,3,2560]{0,2,1:T(8,128)(2,1)} %all-reduce.3.cloned.1.call-done, bf16[640,3,2560]{0,2,1:T(8,128)(2,1)} %copy.27, f32[640,3,8]{0,2,1:T(8,128)S(1)} %rsqrt_multiply_fusion), kind=kLoop, calls=%fused_computation.27 | loop fusion | flops 24576000 | bytes 29552640 | tf_op jit(solution)/shard_map/convert_element_type | solution.py:76
  504.2 6.7 %fusion.35 = f32[8,320,128]{2,1,0:T(8,128)} fusion(bf16[640,8,320]{0,2,1:T(8,128)(2,1)} %bitcast.198, f32[8,640,128]{1,2,0:T(8,128)} %fusion.70, bf16[640,8,320]{0,2,1:T(8,128)(2,1)} %bitcast.197, bf16[128,8,320]{0,2,1:T(8,128)(2,1)S(1)} %bitcast.200), kind=kOutput, calls=%fused_computation.61 | convolution fusion | flops 842792960 | bytes 11141120 | tf_op jit(solution)/shard_map/thj,jhd->thd/dot_general | solution.py:88
  (171 shorter events, 130.5 us)
Async XLA Ops:
  7.4 69.3 %copy-start = (bf16[128,2560]{1,0:T(8,128)(2,1)S(1)}, bf16[128,2560]{1,0:T(8,128)(2,1)}, u32[]{:S(2)}) copy-start(bf16[128,2560]{1,0:T(8,128)(2,1)} %param.10) | copy-start | bytes 1966084
  10.8 11.2 %copy-start.2 = (s32[4096]{0:T(1024)S(1)}, s32[4096]{0:T(1024)}, u32[]{:S(2)}) copy-start(s32[4096]{0:T(1024)} %param.14) | copy-start | bytes 49156
  14.6 50.9 %all-to-all-start.2 = ((bf16[32,4,2560]{2,1,0:T(4,128)(2,1)}), bf16[32,4,2560]{2,1,0:T(4,128)(2,1)S(1)}, u32[]{:S(2)}, u32[]{:S(2)}) async-start(bf16[32,4,2560]{2,1,0:T(4,128)(2,1)} %reshape.104), calls=%async_computation.2 | async-start | bytes 1310720 | tf_op jit(solution)/shard_map/all_to_all | solution.py:134
  21.9 56.8 %sort.52.cloned.1.call-start = ((), (), s32[]{:S(2)}) async-start(), calls=%async_computation.4 | async-start | bytes 98336 | tf_op jit(solution)/shard_map/jit(argsort)/sort | solution.py:137
  30.3 5.7 %copy-start.4 = (bf16[128,2560]{1,0:T(8,128)(2,1)S(1)}, bf16[128,2560]{1,0:T(8,128)(2,1)}, u32[]{:S(2)}) copy-start(bf16[128,2560]{1,0:T(8,128)(2,1)} %param.11) | copy-start | bytes 1966084
  51.1 6.7 %copy-start.11 = (bf16[128,2560]{0,1:T(8,128)(2,1)S(1)}, bf16[128,2560]{0,1:T(8,128)(2,1)}, u32[]{:S(2)}) copy-start(bf16[128,2560]{0,1:T(8,128)(2,1)} %copy.28) | copy-start | bytes 1966084
  51.2 6.7 %copy-start.17 = (f32[128,8]{0,1:T(8,128)S(1)}, f32[128,8]{0,1:T(8,128)}, u32[]{:S(2)}) copy-start(f32[128,8]{0,1:T(8,128)} %param.13) | copy-start | bytes 12292
  57.9 4.6 copy-start.8
  57.9 4.6 copy-start.9
  65.5 43.4 %all-to-all-start.1 = ((bf16[32,4,2560]{2,1,0:T(4,128)(2,1)}), bf16[32,4,2560]{2,1,0:T(4,128)(2,1)S(1)}, u32[]{:S(2)}, u32[]{:S(2)}) async-start(bf16[32,4,2560]{2,1,0:T(4,128)(2,1)} %reshape.102), calls=%async_computation.1 | async-start | bytes 1310720 | tf_op jit(solution)/shard_map/all_to_all | solution.py:133
  79.4 25.6 %copy-start.14 = (s32[32,128]{1,0:T(8,128)S(1)}, s32[32,128]{1,0:T(8,128)}, u32[]{:S(2)}) copy-start(s32[32,128]{1,0:T(8,128)} %get-tuple-element.118) | copy-start | bytes 49156
  109.0 46.6 %all-to-all-start = ((bf16[32,4,2560]{2,1,0:T(4,128)(2,1)}), bf16[32,4,2560]{2,1,0:T(4,128)(2,1)S(1)}, u32[]{:S(2)}, u32[]{:S(2)}) async-start(bf16[32,4,2560]{2,1,0:T(4,128)(2,1)} %reshape.96), calls=%async_computation | async-start | bytes 1310720 | tf_op jit(solution)/shard_map/all_to_all | solution.py:132
  114.8 340.0 %all-reduce.3.cloned.1.call-start = ((), (), s32[]{:S(2)}) async-start(), calls=%async_computation.3 | async-start | bytes 19660800 | tf_op jit(solution)/shard_map/psum | solution.py:147
  117.2 12.5 %copy-start.6 = (bf16[8,640,320]{1,2,0:T(8,128)(2,1)S(1)}, bf16[8,640,320]{1,2,0:T(8,128)(2,1)}, u32[]{:S(2)}) copy-start(bf16[8,640,320]{1,2,0:T(8,128)(2,1)} %convolution_convert_fusion.1) | copy-start | bytes 9830404
  117.2 12.5 %copy-start.7 = (bf16[8,320,640]{2,1,0:T(8,128)(2,1)S(1)}, bf16[8,320,640]{2,1,0:T(8,128)(2,1)}, u32[]{:S(2)}) copy-start(bf16[8,320,640]{2,1,0:T(8,128)(2,1)} %convolution_convert_fusion.2) | copy-start | bytes 9830404
  117.2 111.7 %collective-permute-start = (bf16[2,128,2560]{2,1,0:T(8,128)(2,1)}, bf16[2,128,2560]{2,1,0:T(8,128)(2,1)}, u32[]{:S(2)}, u32[]{:S(2)}) collective-permute-start(bf16[2,128,2560]{2,1,0:T(8,128)(2,1)} %pad_maximum_fusion.1), channel_id=1, source_target_pairs={{0,4},{1,5},{2,6},{3,7},{4,8},{5,9},{6,10},{7,11},{8,12},{9,13},{1... | collective-permute-start | bytes 3932168 | tf_op jit(solution)/shard_map/ppermute | solution.py:20
  125.8 105.8 %collective-permute-start.1 = (bf16[2,128,2560]{2,1,0:T(8,128)(2,1)}, bf16[2,128,2560]{2,1,0:T(8,128)(2,1)}, u32[]{:S(2)}, u32[]{:S(2)}) collective-permute-start(bf16[2,128,2560]{2,1,0:T(8,128)(2,1)} %pad_maximum_fusion.1), channel_id=1, source_target_pairs={{0,3},{1,4},{2,5},{3,6},{4,7},{5,8},{6,9},{7,10},{8,11},{9,12},{10... | collective-permute-start | bytes 3932168 | tf_op jit(solution)/shard_map/ppermute | solution.py:20
  134.4 14.1 %copy-start.15 = (s32[4096]{0:T(1024)S(1)}, s32[4096]{0:T(1024)}, u32[]{:S(2)}) copy-start(s32[4096]{0:T(1024)} %param.15) | copy-start | bytes 49156
  148.7 85.6 %collective-permute-start.2 = (bf16[2,128,2560]{2,1,0:T(8,128)(2,1)}, bf16[2,128,2560]{2,1,0:T(8,128)(2,1)}, u32[]{:S(2)}, u32[]{:S(2)}) collective-permute-start(bf16[2,128,2560]{2,1,0:T(8,128)(2,1)} %pad_maximum_fusion.1), channel_id=1, source_target_pairs={{0,2},{1,3},{2,4},{3,5},{4,6},{5,7},{6,8},{7,9},{8,10},{9,11},{10,... | collective-permute-start | bytes 3932168 | tf_op jit(solution)/shard_map/ppermute | solution.py:20
  152.0 85.0 %collective-permute-start.3 = (bf16[2,128,2560]{2,1,0:T(8,128)(2,1)}, bf16[2,128,2560]{2,1,0:T(8,128)(2,1)}, u32[]{:S(2)}, u32[]{:S(2)}) collective-permute-start(bf16[2,128,2560]{2,1,0:T(8,128)(2,1)} %pad_maximum_fusion.1), channel_id=1, source_target_pairs={{0,1},{1,2},{2,3},{3,4},{4,5},{5,6},{6,7},{7,8},{8,9},{9,10},{10,1... | collective-permute-start | bytes 3932168 | tf_op jit(solution)/shard_map/ppermute | solution.py:20
  154.3 84.2 %collective-permute-start.4 = (bf16[2,128,2560]{2,1,0:T(8,128)(2,1)}, bf16[2,128,2560]{2,1,0:T(8,128)(2,1)}, u32[]{:S(2)}, u32[]{:S(2)}) collective-permute-start(bf16[2,128,2560]{2,1,0:T(8,128)(2,1)} %pad_maximum_fusion.1), channel_id=1, source_target_pairs={{1,0},{2,1},{3,2},{4,3},{5,4},{6,5},{7,6},{8,7},{9,8},{10,9},{11,1... | collective-permute-start | bytes 3932168 | tf_op jit(solution)/shard_map/ppermute | solution.py:20
  228.9 40.4 %collective-permute-start.5 = (bf16[2,128,2560]{2,1,0:T(8,128)(2,1)}, bf16[2,128,2560]{2,1,0:T(8,128)(2,1)S(1)}, u32[]{:S(2)}, u32[]{:S(2)}) collective-permute-start(bf16[2,128,2560]{2,1,0:T(8,128)(2,1)} %pad_maximum_fusion.1), channel_id=1, source_target_pairs={{2,0},{3,1},{4,2},{5,3},{6,4},{7,5},{8,6},{9,7},{10,8},{11,9},{12,... | collective-permute-start | bytes 3932168 | tf_op jit(solution)/shard_map/ppermute | solution.py:20
  231.6 50.2 %collective-permute-start.6 = (bf16[2,128,2560]{2,1,0:T(8,128)(2,1)}, bf16[2,128,2560]{2,1,0:T(8,128)(2,1)S(1)}, u32[]{:S(2)}, u32[]{:S(2)}) collective-permute-start(bf16[2,128,2560]{2,1,0:T(8,128)(2,1)} %pad_maximum_fusion.1), channel_id=1, source_target_pairs={{3,0},{4,1},{5,2},{6,3},{7,4},{8,5},{9,6},{10,7},{11,8},{12,9},{13... | collective-permute-start | bytes 3932168 | tf_op jit(solution)/shard_map/ppermute | solution.py:20
  234.3 62.6 %collective-permute-start.7 = (bf16[2,128,2560]{2,1,0:T(8,128)(2,1)}, bf16[2,128,2560]{2,1,0:T(8,128)(2,1)S(1)}, u32[]{:S(2)}, u32[]{:S(2)}) collective-permute-start(bf16[2,128,2560]{2,1,0:T(8,128)(2,1)} %pad_maximum_fusion.1), channel_id=1, source_target_pairs={{4,0},{5,1},{6,2},{7,3},{8,4},{9,5},{10,6},{11,7},{12,8},{13,9},{1... | collective-permute-start | bytes 3932168 | tf_op jit(solution)/shard_map/ppermute | solution.py:20
  (7 other events, 20.6 us)
Sparse Core Ops, SparseCore 0:
  25.0 3.3 sort.54.cloned.1.call-done
  (1 shorter events, 0.0 us)
Sparse Core Ops, SparseCore 1:
  134.5 320.2 all-reduce.2
where the time goes:
time: 524 us; the launch traced here: 521 us
  waiting for transfers between devices  222 us (42%)
  local copies, waits for them, and re-layouts  95.5 us (18%)
  matrix products  85.7 us (16%)
  other arithmetic  63.1 us (12%)
  starting transfers between devices  38.7 us (7%)
  between operations  15.2 us (3%)
    ppermute x8, waiting for transfers between devices, shifted(): return lax.ppermute(block, axis, route)  129 us
    psum x1, waiting for transfers between devices, shards(): lax.psum(local_grads.astype(jnp.bfloat16), 'tok').astype(jnp.float32)  93.6 us
    dot_general x20, matrix products, one_head(): jnp.einsum('td,sd->ts', query_part, key_part, preferred_element_type=jnp....  29.1 us
    unnamed x48, local copies, waits for them, and re-layouts  28.4 us
    slice x5, local copies, waits for them, and re-layouts, matrix_view(): return weight_rows[:, which].reshape(weight_rows.shape[0], HEADS, HEAD_DIM)  27.3 us
    gather x1, local copies, waits for them, and re-layouts, shards(): arranged = jnp.take_along_axis(all_order, ranked, axis=1)  25.6 us
    dot_general x20, matrix products, one_head(): jnp.dot(weights.astype(jnp.bfloat16), value_part, preferred_element_type=...  25.2 us
    mul x1, other arithmetic, renormed(): anchor * anchor  19.8 us
  transfers between devices with their start and end apart: 12, of which 5 were waited for; matrix products, arithmetic and copies ran while one was open for 33% of the time, Pallas kernels for 0%

commit v1 on v0

v1 whole, which is shorter than its diff:
```python
import functools

import jax
import jax.numpy as jnp
from jax import lax
from jax.experimental import pallas as pl
from jax.experimental.pallas import tpu as pltpu
from jax.sharding import Mesh, PartitionSpec as P

HEADS = 8
ATT_DIM = 128
WINDOW = 1024
SPLIT = 4

epsilon = 1e-06
BF = jnp.bfloat16
F32 = jnp.float32
VM = pl.BlockSpec(memory_space=pltpu.VMEM)
NT = (((1,), (1,)), ((), ()))
TN = (((0,), (0,)), ((), ()))
VMEM_BYTES = 60 * 1024 * 1024


def dot_nt(a, b):
    return lax.dot_general(a, b, NT, preferred_element_type=F32)


def dot_tn(a, b):
    return lax.dot_general(a, b, TN, preferred_element_type=F32)


def dot_nn(a, b):
    return jnp.dot(a, b, preferred_element_type=F32)


def one_hot(left, right):
    return jnp.where(left == right, 1.0, 0.0).astype(BF)


def pack_kernel(span, home, rank_ref, wide_ref, own_ref, query_ref, key_ref, value_ref, out_ref):
    rank = rank_ref[...]
    wide = one_hot(wide_ref[...], rank)
    own = one_hot(own_ref[...], rank)
    groups, width = out_ref.shape[0], out_ref.shape[3]
    keys = dot_nn(wide, key_ref[...]).astype(BF)
    values = dot_nn(wide, value_ref[...]).astype(BF)
    rows = dot_nn(own, query_ref[...]).astype(BF)
    out_ref[:, 0, 0:span, :] = keys.reshape(groups, span, width)
    out_ref[:, 0, span : 2 * span, :] = values.reshape(groups, span, width)
    out_ref[:, 0, 2 * span :, :] = rows.reshape(groups, home, width)


def grads_kernel(span, home, head_dim, recv_ref, rate_ref, weight_ref, out_ref):
    count, _, width = recv_ref.shape
    tokens = count * home
    keys = recv_ref[:, home : 2 * home, :].reshape(tokens, width)
    values = recv_ref[:, span + home : span + 2 * home, :].reshape(tokens, width).astype(F32)
    column = lax.broadcasted_iota(jnp.int32, (1, width), 1)
    for which in range(width // head_dim):
        inside = (column >= which * head_dim) & (column < (which + 1) * head_dim)
        key_part = jnp.where(inside, keys.astype(F32), 0.0).astype(BF)
        target = jnp.where(inside, values * rate_ref[:, which : which + 1], 0.0).astype(BF)
        gate = dot_nt(key_part, weight_ref[0])
        upward = dot_nt(key_part, weight_ref[1])
        backward = dot_nt(target, weight_ref[2])
        sigmoid = jax.nn.sigmoid(gate)
        active = gate * sigmoid
        product = (active * upward).astype(BF)
        delta_gate = (backward * upward * sigmoid * (1.0 + gate * (1.0 - sigmoid))).astype(BF)
        delta_upper = (backward * active).astype(BF)
        parts = (
            dot_tn(delta_gate, key_part),
            dot_tn(delta_upper, key_part),
            dot_tn(product, target),
        )
        for matrix, part in enumerate(parts):
            if which == 0:
                out_ref[matrix] = part.astype(BF)
            else:
                out_ref[matrix] = jnp.where(inside, part, out_ref[matrix].astype(F32)).astype(BF)


def attend_kernel(span, home, chunk, recv_ref, kpos_ref, qpos_ref, low_ref, high_ref, begin_ref, out_ref, query_ref):
    count, _, width = recv_ref.shape
    tokens = count * home
    keys = recv_ref[:, 0:span, :].reshape(count * span, width)
    values = recv_ref[:, span : 2 * span, :].reshape(count * span, width)
    arrived = recv_ref[:, 2 * span :, :].reshape(tokens, width)
    kpos = kpos_ref[...]
    qpos = qpos_ref[...]
    for start in range(0, tokens, chunk):
        place = begin_ref[start : start + chunk, :]
        query = dot_nn(one_hot(place, qpos), arrived).astype(BF)
        query_ref[start : start + chunk, :] = query
        scores = dot_nt(query, keys) * ATT_DIM ** (-0.5)
        allowed = (kpos >= low_ref[start : start + chunk, :]) & (
            kpos < high_ref[start : start + chunk, :]
        )
        scores = jnp.where(allowed, scores, -1e30)
        peak = jnp.max(scores, axis=1, keepdims=True)
        weights = jnp.exp(scores - peak)
        total = jnp.sum(weights, axis=1, keepdims=True)
        out_ref[start : start + chunk, :] = dot_nn(weights.astype(BF), values) / total


def apply_kernel(head_dim, query_ref, weight_ref, grad_ref, attended_ref, out_ref):
    width = query_ref.shape[1]
    column = lax.broadcasted_iota(jnp.int32, (1, width), 1)
    insides = [
        (column >= which * head_dim) & (column < (which + 1) * head_dim)
        for which in range(width // head_dim)
    ]
    fresh = []
    for matrix in range(3):
        base = weight_ref[matrix].astype(F32)
        update = base + grad_ref[matrix].astype(F32)
        base_square = base * base
        update_square = update * update
        scaling = jnp.zeros_like(update)
        for inside in insides:
            old = jnp.sum(jnp.where(inside, base_square, 0.0), axis=1, keepdims=True)
            new = jnp.sum(jnp.where(inside, update_square, 0.0), axis=1, keepdims=True)
            ratio = jnp.sqrt(old + epsilon) / jnp.sqrt(new + epsilon)
            scaling = jnp.where(inside, ratio, scaling)
        fresh.append((update * scaling).astype(BF))
    query = query_ref[...].astype(F32)
    result = attended_ref[...]
    for inside in insides:
        query_part = jnp.where(inside, query, 0.0).astype(BF)
        gate = dot_nt(query_part, fresh[0])
        upward = dot_nt(query_part, fresh[1])
        product = (gate * jax.nn.sigmoid(gate) * upward).astype(BF)
        result = result + jnp.where(inside, dot_nn(product, fresh[2]), 0.0)
    out_ref[...] = result.astype(BF)


def norm_kernel(part_ref, gain_ref, out_ref):
    count, _, width = part_ref.shape
    square = 0.0
    for index in range(count):
        part = part_ref[index].astype(F32)
        square = square + jnp.sum(part * part, axis=1, keepdims=True)
    scale = lax.rsqrt(square / (count * width) + epsilon)
    for index in range(count):
        columns = slice(index * width, (index + 1) * width)
        out_ref[:, columns] = (
            part_ref[index].astype(F32) * scale * gain_ref[:, columns]
        ).astype(BF)


def call(kernel, name, out_shape, flops, size, **options):
    return pl.pallas_call(
        kernel,
        name=name,
        out_shape=out_shape,
        compiler_params=pltpu.CompilerParams(vmem_limit_bytes=VMEM_BYTES),
        cost_estimate=pl.CostEstimate(flops=flops, bytes_accessed=size, transcendentals=0),
        **options,
    )


def shards(
    queries, key_rows, value_rows, learn_rates, frame_order, window_ids, fast_init, norm_gain
):
    tok_dev, model = queries.shape
    groups = lax.axis_size("seg")
    sections = groups * SPLIT
    group = lax.axis_index("seg")
    part = lax.axis_index("hd")
    rank_own = group * SPLIT + part
    slots = tok_dev // sections
    half = WINDOW // 2
    home = SPLIT * slots
    reach = -(-half // tok_dev) * slots
    span = home + 2 * reach
    assert reach == home
    width = model // SPLIT
    head_dim = model // HEADS
    hidden = fast_init.shape[0]
    tokens = sections * home
    counter = jnp.arange(tok_dev, dtype=jnp.int32)

    order = frame_order.reshape(sections, tok_dev)
    sort_key = order // tok_dev * tok_dev + counter[None, :]
    ranks = jnp.sum(
        (sort_key[:, None, :] < sort_key[:, :, None]).astype(jnp.int32), axis=2
    )
    own_rank = lax.dynamic_slice_in_dim(ranks, rank_own, 1, 0)

    wide_want = (
        jnp.arange(groups, dtype=jnp.int32)[:, None] * home
        - reach
        + jnp.arange(span, dtype=jnp.int32)[None, :]
    ).reshape(-1, 1)
    send = call(
        functools.partial(pack_kernel, span, home),
        "pack",
        jax.ShapeDtypeStruct((groups, SPLIT, 2 * span + home, width), BF),
        2 * (2 * groups * span + tok_dev) * tok_dev * model,
        2 * model * (3 * tok_dev + groups * (2 * span + home)),
        grid=(SPLIT,),
        in_specs=[
            pl.BlockSpec((1, tok_dev), lambda h: (0, 0)),
            pl.BlockSpec((groups * span, 1), lambda h: (0, 0)),
            pl.BlockSpec((tok_dev, 1), lambda h: (0, 0)),
            pl.BlockSpec((tok_dev, width), lambda h: (0, h)),
            pl.BlockSpec((tok_dev, width), lambda h: (0, h)),
            pl.BlockSpec((tok_dev, width), lambda h: (0, h)),
        ],
        out_specs=pl.BlockSpec((groups, 1, 2 * span + home, width), lambda h: (0, h, 0, 0)),
    )(own_rank, wide_want, counter[:, None], queries, key_rows, value_rows)
    recv = lax.all_to_all(
        send.reshape(sections, 2 * span + home, width),
        ("seg", "hd"),
        split_axis=0,
        concat_axis=0,
        tiled=True,
    )

    sorting = (own_rank == counter[:, None]).astype(F32)
    rates = jnp.dot(sorting, learn_rates, precision=lax.Precision.HIGHEST)
    rates = rates.reshape(groups, home, SPLIT, HEADS // SPLIT).transpose(0, 2, 1, 3)
    rates = lax.all_to_all(
        rates.reshape(sections, home, HEADS // SPLIT),
        ("seg", "hd"),
        split_axis=0,
        concat_axis=0,
        tiled=True,
    ).reshape(tokens, HEADS // SPLIT)

    wanted = group * home - reach + jnp.arange(span, dtype=jnp.int32)
    match = ranks[:, None, :] == wanted[None, :, None]
    positions = jnp.max(jnp.where(match, order[:, None, :], -1), axis=2)
    kpos = positions.reshape(1, sections * span)
    qpos = positions[:, reach : reach + home].reshape(1, tokens)
    first = group * tokens
    place = first + jnp.arange(tokens, dtype=jnp.int32)
    ids = lax.dynamic_slice_in_dim(window_ids, first, tokens, 0)
    clip_low = jnp.sum((window_ids[None, :] < ids[:, None]).astype(jnp.int32), axis=1)
    clip_high = jnp.sum((window_ids[None, :] <= ids[:, None]).astype(jnp.int32), axis=1)
    low = jnp.maximum(clip_low, place - (half - 1))[:, None]
    high = jnp.minimum(clip_high, place + half)[:, None]

    weight = lax.dynamic_slice_in_dim(fast_init, part * width, width, 2).transpose(1, 0, 2)
    grads = call(
        functools.partial(grads_kernel, span, home, head_dim),
        "grads",
        jax.ShapeDtypeStruct((3, hidden, width), BF),
        24 * tokens * hidden * width,
        4 * tokens * width + 12 * hidden * width,
        in_specs=[VM] * 3,
        out_specs=VM,
    )(recv, rates, weight)
    grads = lax.psum(grads, "seg")

    whole = lambda h: (0, 0)
    attended, query_seq = call(
        functools.partial(attend_kernel, span, home, min(tokens, 128)),
        "attend",
        (
            jax.ShapeDtypeStruct((tokens, width), F32),
            jax.ShapeDtypeStruct((tokens, width), BF),
        ),
        8 * tokens * sections * span * width,
        2 * sections * (2 * span + home) * width + 6 * tokens * width,
        grid=(width // ATT_DIM,),
        in_specs=[
            pl.BlockSpec((sections, 2 * span + home, ATT_DIM), lambda h: (0, 0, h)),
            pl.BlockSpec((1, sections * span), whole),
            pl.BlockSpec((1, tokens), whole),
            pl.BlockSpec((tokens, 1), whole),
            pl.BlockSpec((tokens, 1), whole),
            pl.BlockSpec((tokens, 1), whole),
        ],
        out_specs=(
            pl.BlockSpec((tokens, ATT_DIM), lambda h: (0, h)),
            pl.BlockSpec((tokens, ATT_DIM), lambda h: (0, h)),
        ),
    )(recv, kpos, qpos, low, high, place[:, None])

    combined = call(
        functools.partial(apply_kernel, head_dim),
        "apply",
        jax.ShapeDtypeStruct((tokens, width), BF),
        12 * tokens * hidden * width,
        8 * tokens * width + 12 * hidden * width,
        in_specs=[VM] * 4,
        out_specs=VM,
    )(query_seq, weight, grads, attended)
    returned = lax.all_to_all(
        combined.reshape(SPLIT, tok_dev, width), "hd", split_axis=0, concat_axis=0, tiled=True
    )
    return call(
        norm_kernel,
        "norm",
        jax.ShapeDtypeStruct((tok_dev, model), BF),
        8 * tok_dev * model,
        4 * tok_dev * model,
        in_specs=[VM] * 2,
        out_specs=VM,
    )(returned, norm_gain[None, :])


def solution(mesh):
    count = mesh.shape["tok"]
    split_mesh = Mesh(
        mesh.devices.reshape(mesh.shape["groups"], count // SPLIT, SPLIT),
        ("groups", "seg", "hd"),
    )
    rows = P(("groups", "seg", "hd"), None)
    return jax.shard_map(
        shards,
        mesh=split_mesh,
        in_specs=(rows, rows, rows, rows, P("groups"), P("groups"), P(), P()),
        out_specs=rows,
        check_vma=False,
    )
```

time: 524 us -> 289 us (0.55)
  matrix products: 85.7 us -> 0.12 us
  local copies, waits for them, and re-layouts: 95.5 us -> 11 us
  other arithmetic: 63.1 us -> 6.39 us
  Pallas kernels: 0 us -> 44.7 us
  waiting for transfers between devices: 222 us -> 196 us
  starting transfers between devices: 38.7 us -> 16.8 us
    ppermute x8 -> x0, waiting for transfers between devices: 129 us -> none  [shifted(): return lax.ppermute(block, axis, route)]
    all_to_all x3, waiting for transfers between devices: 0.01 us -> 107 us  [the longest x1 97.9 us: shards(): lax.all_to_all(send.reshape(sections, 2 * span + home, width), ('seg', 'h...]
    dot_general x48 -> x1, matrix products: 85.7 us -> 0.12 us  [shards(): rates = jnp.dot(sorting, learn_rates, precision=lax.Precision.HIGHEST)]
    pallas_call x0 -> x5, Pallas kernels: none -> 44.7 us  [the longest x1 15.3 us: shards(): call(functools.partial(attend_kernel, span, home, min(tokens, 128)), 'att...]
    gather x8 -> x0, local copies, waits for them, and re-layouts: 33.6 us -> none  [the longest x1 25.6 us: shards(): arranged = jnp.take_along_axis(all_order, ranked, axis=1)]
    slice x5 -> x1, local copies, waits for them, and re-layouts: 27.3 us -> 0.07 us  [shards(): qpos = positions[:, reach:reach + home].reshape(1, tokens)]
    unnamed x48 -> x10, local copies, waits for them, and re-layouts: 28.4 us -> 1.52 us
    mul x1 -> x0, other arithmetic: 19.8 us -> none  [renormed(): anchor * anchor]
  transfers between devices with their start and end apart: 12 -> 4, of which waited for: 5 -> 3; matrix products, arithmetic and copies ran while one was open for 33% -> 5% of each run, Pallas kernels for 0% -> 7%
where the time goes in v1:
time: 289 us; the launch traced here: 288 us
  waiting for transfers between devices  196 us (68%)
  Pallas kernels  44.7 us (15%)
  starting transfers between devices  16.8 us (6%)
  between operations  13.5 us (5%)
  local copies, waits for them, and re-layouts  11 us (4%)
  other arithmetic  6.39 us (2%)
    all_to_all x1, waiting for transfers between devices, shards(): lax.all_to_all(send.reshape(sections, 2 * span + home, width), ('seg', 'h...  97.9 us
    psum x1, waiting for transfers between devices, shards(): grads = lax.psum(grads, 'seg')  88.5 us
    pallas_call x1, Pallas kernels, shards(): call(functools.partial(attend_kernel, span, home, min(tokens, 128)), 'att...  15.3 us
    pallas_call x1, Pallas kernels, shards(): call(functools.partial(grads_kernel, span, home, head_dim), 'grads', jax....  11.9 us
    pallas_call x1, Pallas kernels, shards(): call(functools.partial(apply_kernel, head_dim), 'apply', jax.ShapeDtypeSt...  9.68 us
    all_to_all x1, waiting for transfers between devices, shards(): lax.all_to_all(combined.reshape(SPLIT, tok_dev, width), 'hd', split_axis=...  9.57 us
    all_to_all x1, starting transfers between devices, shards(): lax.all_to_all(rates.reshape(sections, home, HEADS // SPLIT), ('seg', 'hd...  7.33 us
    all_to_all x1, starting transfers between devices, shards(): lax.all_to_all(send.reshape(sections, 2 * span + home, width), ('seg', 'h...  5.95 us
  transfers between devices with their start and end apart: 4, of which 3 were waited for; matrix products, arithmetic and copies ran while one was open for 5% of the time, Pallas kernels for 7%

profile of v1, /device:TPU:0, one launch (start us, length us, event | category | flops | bytes accessed | tf_op | source)
XLA Modules:
  0.0 288.5 jit_solution(4400016058827354940)
XLA Ops:
  6.5 0.7 fusion.4
  7.3 1.3 convert_reduce_fusion.2
  8.8 0.7 copy.28
  9.5 7.3 %all-to-all-start.1 = ((f32[32,16,2]{1,2,0:T(2,128)}), f32[32,16,2]{1,2,0:T(2,128)S(1)}, u32[]{:S(2)}, u32[]{:S(2)}) async-start(f32[32,16,2]{1,2,0:T(2,128)} %bitcast.7), calls=%async_computation.1 | async-start | bytes 65536 | tf_op jit(solution)/shard_map/all_to_all | solution.py:223
  17.5 0.8 add.137.wide_ref
  18.9 5.5 %pack.1 = bf16[8,4,112,640]{3,2,1,0:T(8,128)(2,1)} custom-call(s32[1,128]{1,0:T(1,128)} %constant_dynamic-slice_fusion.rank_ref, s32[384,1]{1,0:T(8,128)} %add.137.wide_ref, s32[128,1]{1,0:T(8,128)} %iota.37.own_ref, bf16[128,2560]{1,0:T(8,128)(2,1)} %query_ref.1, bf16[128,2560]{1,0:T(8,128)(2,1)} %key_ref.1, bf16[128,2560]{1,0:T(8,128)(2,1)} %value_ref.1), custom_call_target="tpu_custom_call" | custom-call | flops 587202560 | bytes 6553600 | tf_op jit(solution)/shard_map/pack/pallas_call | solution.py:195
  24.4 5.9 %all-to-all-start = ((bf16[32,112,640]{2,1,0:T(8,128)(2,1)}), bf16[32,112,640]{2,1,0:T(8,128)(2,1)}, u32[]{:S(2)}, u32[]{:S(2)}) async-start(bf16[32,112,640]{2,1,0:T(8,128)(2,1)} %bitcast.16), calls=%async_computation | async-start | bytes 9175040 | tf_op jit(solution)/shard_map/all_to_all | solution.py:212
  30.4 3.4 %dynamic-slice_bitcast_fusion.weight_ref = bf16[3,640,640]{2,1,0:T(8,128)(2,1)} fusion(bf16[640,3,2560]{2,0,1:T(8,128)(2,1)} %param.14, s32[]{:T(128)S(6)} %select_n.30), kind=kLoop, calls=%fused_computation.2 | loop fusion | bytes 4915204 | tf_op jit(solution)/shard_map/transpose | solution.py:244
  33.8 1.0 copy.29
  34.7 97.9 %all-to-all-done.recv_ref = bf16[32,112,640]{2,1,0:T(8,128)(2,1)} async-done(((bf16[32,112,640]{2,1,0:T(8,128)(2,1)}), bf16[32,112,640]{2,1,0:T(8,128)(2,1)}, u32[]{:S(2)}, u32[]{:S(2)}) %all-to-all-start) | async-done | bytes 4587552 | tf_op jit(solution)/shard_map/all_to_all | solution.py:212
  132.6 11.9 %grads.1 = bf16[3,640,640]{2,1,0:T(8,128)(2,1)} custom-call(bf16[32,112,640]{2,1,0:T(8,128)(2,1)} %all-to-all-done.recv_ref, f32[512,2]{1,0:T(8,128)} %bitcast.18, bf16[3,640,640]{2,1,0:T(8,128)(2,1)} %dynamic-slice_bitcast_fusion.weight_ref), custom_call_target="tpu_custom_call" | custom-call | flops 5033164800 | bytes 6225920 | tf_op jit(solution)/shard_map/grads/pallas_call | solution.py:245
  144.6 0.7 copy-done.2
  145.3 0.7 select_reduce_fusion
  146.0 0.7 reshape.163.kpos_ref
  146.8 2.0 convert_reduce_fusion
  149.8 0.7 iota_add_fusion.begin_ref
  150.5 0.9 add_minimum_fusion
  151.4 15.3 %attend.1 = (f32[512,640]{1,0:T(8,128)}, bf16[512,640]{1,0:T(8,128)(2,1)}) custom-call(bf16[32,112,640]{2,1,0:T(8,128)(2,1)} %all-to-all-done.recv_ref, s32[1,1536]{1,0:T(1,128)} %reshape.163.kpos_ref, s32[1,512]{1,0:T(1,128)} %reshape.164.qpos_ref, s32[512,1]{1,0:T(8,128)} %get-tuple-element.12.low_ref, s32[512,1]{1,0:T(8,128)} %get-tuple-element.11.high_ref, ...), custom_call_target="tpu_custom_call" | custom-call | flops 4026531840 | bytes 6553600 | tf_op jit(solution)/shard_map/attend/pallas_call | solution.py:257
  166.7 88.5 %all-reduce.2.cloned.1.call-done.grad_ref = bf16[3,640,640]{2,1,0:T(8,128)(2,1)} async-done(((bf16[3,640,640]{2,1,0:T(8,128)(2,1)}), bf16[3,640,640]{2,1,0:T(8,128)(2,1)}) %all-reduce.2.cloned.1.call-update) | async-done | bytes 2457616 | tf_op jit(solution)/shard_map/psum | solution.py:254
  255.2 9.7 %apply.1 = bf16[512,640]{1,0:T(8,128)(2,1)} custom-call(bf16[512,640]{1,0:T(8,128)(2,1)} %get-tuple-element.7.query_ref, bf16[3,640,640]{2,1,0:T(8,128)(2,1)} %dynamic-slice_bitcast_fusion.weight_ref, bf16[3,640,640]{2,1,0:T(8,128)(2,1)} %all-reduce.2.cloned.1.call-done.grad_ref, f32[512,640]{1,0:T(8,128)} %get-tuple-element.8.attended_ref), custom_call_target="tpu_custom_call" | custom-call | flops 2516582400 | bytes 7536640 | tf_op jit(solution)/shard_map/apply/pallas_call | solution.py:281
  264.9 3.5 %all-to-all-start.2 = ((bf16[4,128,640]{2,1,0:T(8,128)(2,1)}), bf16[4,128,640]{2,1,0:T(8,128)(2,1)S(1)}, u32[]{:S(2)}, u32[]{:S(2)}) async-start(bf16[4,128,640]{2,1,0:T(8,128)(2,1)} %bitcast.17), calls=%async_computation.2 | async-start | bytes 1310720 | tf_op jit(solution)/shard_map/all_to_all | solution.py:290
  269.0 9.6 %all-to-all-done.2.part_ref = bf16[4,128,640]{2,1,0:T(8,128)(2,1)S(1)} async-done(((bf16[4,128,640]{2,1,0:T(8,128)(2,1)}), bf16[4,128,640]{2,1,0:T(8,128)(2,1)S(1)}, u32[]{:S(2)}, u32[]{:S(2)}) %all-to-all-start.2) | async-done | bytes 655392 | tf_op jit(solution)/shard_map/all_to_all | solution.py:290
  278.5 0.8 copy-done.1
  279.4 2.3 norm.1
  (25 shorter events, 3.3 us)
Async XLA Ops:
  6.5 2.1 copy-start
  9.5 14.9 %all-to-all-start.1 = ((f32[32,16,2]{1,2,0:T(2,128)}), f32[32,16,2]{1,2,0:T(2,128)S(1)}, u32[]{:S(2)}, u32[]{:S(2)}) async-start(f32[32,16,2]{1,2,0:T(2,128)} %bitcast.7), calls=%async_computation.1 | async-start | bytes 65536 | tf_op jit(solution)/shard_map/all_to_all | solution.py:223
  24.4 108.2 %all-to-all-start = ((bf16[32,112,640]{2,1,0:T(8,128)(2,1)}), bf16[32,112,640]{2,1,0:T(8,128)(2,1)}, u32[]{:S(2)}, u32[]{:S(2)}) async-start(bf16[32,112,640]{2,1,0:T(8,128)(2,1)} %bitcast.16), calls=%async_computation | async-start | bytes 9175040 | tf_op jit(solution)/shard_map/all_to_all | solution.py:212
  30.4 224.8 %all-reduce.2.cloned.1.call-start = ((), (), s32[]{:S(2)}) async-start(), calls=%async_computation.3 | async-start | bytes 4915200 | tf_op jit(solution)/shard_map/psum | solution.py:254
  144.6 0.7 copy-start.2
  144.6 2.2 copy-start.4
  255.2 13.2 %copy-start.3 = (f32[2560]{0:T(1024)S(1)}, f32[2560]{0:T(1024)}, u32[]{:S(2)}) copy-start(f32[2560]{0:T(1024)} %param.15) | copy-start | bytes 30724
  264.9 13.7 %all-to-all-start.2 = ((bf16[4,128,640]{2,1,0:T(8,128)(2,1)}), bf16[4,128,640]{2,1,0:T(8,128)(2,1)S(1)}, u32[]{:S(2)}, u32[]{:S(2)}) async-start(bf16[4,128,640]{2,1,0:T(8,128)(2,1)} %bitcast.17), calls=%async_computation.2 | async-start | bytes 1310720 | tf_op jit(solution)/shard_map/all_to_all | solution.py:290
  278.5 0.8 copy-start.1
Sparse Core Ops, SparseCore 0:
  144.7 110.4 all-reduce.1
